TPU v7x, 32 devices: a whole 2x2x4 slice. The times are simulated.
32 devices in a mesh: dp: 32 (over z, y, x, core).
Axes of the slice: x: 2, y: 2, z: 4, core: 2. Of those that a mesh axis runs over, the one named last changes fastest.
Arguments:
- img_emb: bfloat16 [32768, 512], P('dp')
- txt_emb: bfloat16 [32768, 512], P('dp')
- log_temp: float32 [], replicated
- logit_bias: float32 [], replicated
Outputs:
- output 1: float32 [], replicated
- output 2: float32 [32768, 512], P('dp')
- output 3: float32 [32768, 512], P('dp')
- output 4: float32 [], replicated
- output 5: float32 [], replicated
All inputs are finite; a program needn't handle non-finite values.
Results may differ from a plain program's by a relative error of at most 0.001.
Values are sent between devices in bfloat16 or wider.
A program may use at most 1 GiB of HBM per device.

v0:
```python
import jax
import jax.numpy as jnp
from jax import lax
from jax.sharding import PartitionSpec as P


def normalize_rows(emb):
    emb32 = emb.astype(jnp.float32)
    inv_norm = lax.rsqrt(jnp.sum(emb32 * emb32, axis=-1, keepdims=True))
    return emb32 * inv_norm, inv_norm


def project_back(unit_rows, inv_norm, grad_dir):
    radial = jnp.sum(unit_rows * grad_dir, axis=-1, keepdims=True)
    return (grad_dir - unit_rows * radial) * inv_norm


def pair_terms(img_b, txt_blk, temp_scale, logit_bias, label_signs):
    sim_vals = jnp.einsum('id,jd->ij', img_b, txt_blk, preferred_element_type=jnp.float32)
    logits = temp_scale * sim_vals + logit_bias
    weights = -label_signs * jax.nn.sigmoid(-label_signs * logits)
    weights_b = weights.astype(jnp.bfloat16)
    img_part = jnp.einsum('ij,jd->id', weights_b, txt_blk, preferred_element_type=jnp.float32)
    txt_part = jnp.einsum('ij,id->jd', weights_b, img_b, preferred_element_type=jnp.float32)
    stat_sums = jnp.stack([
        jnp.sum(jax.nn.softplus(-label_signs * logits)),
        jnp.sum(weights),
        jnp.sum(weights * sim_vals),
    ])
    return img_part, txt_part, stat_sums


def solution(mesh):
    group_size = mesh.shape['dp']
    shift_pairs = [(src_dev, (src_dev + 1) % group_size) for src_dev in range(group_size)]

    def local_fn(img_emb, txt_emb, log_temp, logit_bias):
        rows_dev = img_emb.shape[0]
        total_rows = rows_dev * group_size
        img_unit, img_inv = normalize_rows(img_emb)
        txt_unit, txt_inv = normalize_rows(txt_emb)
        img_b = img_unit.astype(jnp.bfloat16)
        txt_b = txt_unit.astype(jnp.bfloat16)
        temp_scale = jnp.exp(log_temp)
        local_ids = jnp.arange(rows_dev)
        diag_signs = jnp.where(local_ids[:, None] == local_ids[None, :], 1.0, -1.0)
        img_acc, txt_acc, stat_sums = pair_terms(img_b, txt_b, temp_scale, logit_bias, diag_signs)

        def visit_step(step_idx, loop_state):
            txt_blk, txt_acc, img_acc, stat_sums = loop_state
            txt_blk = lax.ppermute(txt_blk, 'dp', shift_pairs)
            txt_acc = lax.ppermute(txt_acc, 'dp', shift_pairs)
            img_part, txt_part, new_sums = pair_terms(img_b, txt_blk, temp_scale, logit_bias, -1.0)
            return txt_blk, txt_acc + txt_part, img_acc + img_part, stat_sums + new_sums

        loop_state = lax.fori_loop(0, group_size - 1, visit_step, (txt_b, txt_acc, img_acc, stat_sums))
        txt_acc = lax.ppermute(loop_state[1], 'dp', shift_pairs)
        img_acc = loop_state[2]
        stat_sums = lax.psum(loop_state[3], 'dp') / total_rows
        grad_img = project_back(img_unit, img_inv, temp_scale * img_acc)
        grad_txt = project_back(txt_unit, txt_inv, temp_scale * txt_acc)
        return stat_sums[0], grad_img, grad_txt, temp_scale * stat_sums[2], stat_sums[1]

    return jax.shard_map(
        local_fn,
        mesh=mesh,
        in_specs=(P('dp', None), P('dp', None), P(), P()),
        out_specs=(P(), P('dp', None), P('dp', None), P(), P()),
        check_vma=False,
    )
```

profile of v0, /device:TPU:0, one launch (start us, length us, event | category | flops | bytes accessed | tf_op | source)
XLA Modules:
  0.0 1481.5 jit_solution(17037280513422512624)
XLA Ops:
  19.4 1401.8 %while.16 = (s32[]{:T(128)}, bf16[1024,512]{1,0:T(8,128)(2,1)}, f32[1024,512]{1,0:T(8,128)}, f32[1024,512]{1,0:T(8,128)}, f32[3]{0:T(128)S(1)}, /*index=5*/f32[]...) while((s32[]{:T(128)}, bf16[1024,512]{1,0:T(8,128)(2,1)}, f32[1024,512]{1,0:T(8,128)}, ...), condition=%wide.region_9.10_spmd, body=%wide.region_5.9_spmd.sunk | while | flops 3250585600 | bytes 56623404 | solution.py:56
  22.5 15.8 %collective-permute-done = bf16[1024,512]{1,0:T(8,128)(2,1)S(1)} collective-permute-done((bf16[1024,512]{1,0:T(8,128)(2,1)}, bf16[1024,512]{1,0:T(8,128)(2,1)S(1)}, u32[]{:S(2)}, u32[]{:S(2)}) %collective-permute-start) | collective-permute-done | bytes 1048608 | tf_op jit(solution)/shard_map/while/body/eval_jaxpr/ppermute | solution.py:51
  49.5 11.3 collective-permute-done.1
  65.7 17.8 %collective-permute-done = bf16[1024,512]{1,0:T(8,128)(2,1)S(1)} collective-permute-done((bf16[1024,512]{1,0:T(8,128)(2,1)}, bf16[1024,512]{1,0:T(8,128)(2,1)S(1)}, u32[]{:S(2)}, u32[]{:S(2)}) %collective-permute-start) | collective-permute-done | bytes 1048608 | tf_op jit(solution)/shard_map/while/body/eval_jaxpr/ppermute | solution.py:51
  110.9 17.8 %collective-permute-done = bf16[1024,512]{1,0:T(8,128)(2,1)S(1)} collective-permute-done((bf16[1024,512]{1,0:T(8,128)(2,1)}, bf16[1024,512]{1,0:T(8,128)(2,1)S(1)}, u32[]{:S(2)}, u32[]{:S(2)}) %collective-permute-start) | collective-permute-done | bytes 1048608 | tf_op jit(solution)/shard_map/while/body/eval_jaxpr/ppermute | solution.py:51
  156.1 17.8 %collective-permute-done = bf16[1024,512]{1,0:T(8,128)(2,1)S(1)} collective-permute-done((bf16[1024,512]{1,0:T(8,128)(2,1)}, bf16[1024,512]{1,0:T(8,128)(2,1)S(1)}, u32[]{:S(2)}, u32[]{:S(2)}) %collective-permute-start) | collective-permute-done | bytes 1048608 | tf_op jit(solution)/shard_map/while/body/eval_jaxpr/ppermute | solution.py:51
  185.1 11.3 collective-permute-done.1
  201.3 17.8 %collective-permute-done = bf16[1024,512]{1,0:T(8,128)(2,1)S(1)} collective-permute-done((bf16[1024,512]{1,0:T(8,128)(2,1)}, bf16[1024,512]{1,0:T(8,128)(2,1)S(1)}, u32[]{:S(2)}, u32[]{:S(2)}) %collective-permute-start) | collective-permute-done | bytes 1048608 | tf_op jit(solution)/shard_map/while/body/eval_jaxpr/ppermute | solution.py:51
  230.3 11.3 collective-permute-done.1
  246.4 17.8 %collective-permute-done = bf16[1024,512]{1,0:T(8,128)(2,1)S(1)} collective-permute-done((bf16[1024,512]{1,0:T(8,128)(2,1)}, bf16[1024,512]{1,0:T(8,128)(2,1)S(1)}, u32[]{:S(2)}, u32[]{:S(2)}) %collective-permute-start) | collective-permute-done | bytes 1048608 | tf_op jit(solution)/shard_map/while/body/eval_jaxpr/ppermute | solution.py:51
  275.4 11.3 collective-permute-done.1
  291.6 17.8 %collective-permute-done = bf16[1024,512]{1,0:T(8,128)(2,1)S(1)} collective-permute-done((bf16[1024,512]{1,0:T(8,128)(2,1)}, bf16[1024,512]{1,0:T(8,128)(2,1)S(1)}, u32[]{:S(2)}, u32[]{:S(2)}) %collective-permute-start) | collective-permute-done | bytes 1048608 | tf_op jit(solution)/shard_map/while/body/eval_jaxpr/ppermute | solution.py:51
  336.8 17.8 %collective-permute-done = bf16[1024,512]{1,0:T(8,128)(2,1)S(1)} collective-permute-done((bf16[1024,512]{1,0:T(8,128)(2,1)}, bf16[1024,512]{1,0:T(8,128)(2,1)S(1)}, u32[]{:S(2)}, u32[]{:S(2)}) %collective-permute-start) | collective-permute-done | bytes 1048608 | tf_op jit(solution)/shard_map/while/body/eval_jaxpr/ppermute | solution.py:51
  382.0 17.8 %collective-permute-done = bf16[1024,512]{1,0:T(8,128)(2,1)S(1)} collective-permute-done((bf16[1024,512]{1,0:T(8,128)(2,1)}, bf16[1024,512]{1,0:T(8,128)(2,1)S(1)}, u32[]{:S(2)}, u32[]{:S(2)}) %collective-permute-start) | collective-permute-done | bytes 1048608 | tf_op jit(solution)/shard_map/while/body/eval_jaxpr/ppermute | solution.py:51
  411.0 11.3 collective-permute-done.1
  427.2 17.8 %collective-permute-done = bf16[1024,512]{1,0:T(8,128)(2,1)S(1)} collective-permute-done((bf16[1024,512]{1,0:T(8,128)(2,1)}, bf16[1024,512]{1,0:T(8,128)(2,1)S(1)}, u32[]{:S(2)}, u32[]{:S(2)}) %collective-permute-start) | collective-permute-done | bytes 1048608 | tf_op jit(solution)/shard_map/while/body/eval_jaxpr/ppermute | solution.py:51
  456.2 11.3 collective-permute-done.1
  472.3 17.8 %collective-permute-done = bf16[1024,512]{1,0:T(8,128)(2,1)S(1)} collective-permute-done((bf16[1024,512]{1,0:T(8,128)(2,1)}, bf16[1024,512]{1,0:T(8,128)(2,1)S(1)}, u32[]{:S(2)}, u32[]{:S(2)}) %collective-permute-start) | collective-permute-done | bytes 1048608 | tf_op jit(solution)/shard_map/while/body/eval_jaxpr/ppermute | solution.py:51
  501.3 11.3 collective-permute-done.1
  517.5 17.8 %collective-permute-done = bf16[1024,512]{1,0:T(8,128)(2,1)S(1)} collective-permute-done((bf16[1024,512]{1,0:T(8,128)(2,1)}, bf16[1024,512]{1,0:T(8,128)(2,1)S(1)}, u32[]{:S(2)}, u32[]{:S(2)}) %collective-permute-start) | collective-permute-done | bytes 1048608 | tf_op jit(solution)/shard_map/while/body/eval_jaxpr/ppermute | solution.py:51
  562.7 17.8 %collective-permute-done = bf16[1024,512]{1,0:T(8,128)(2,1)S(1)} collective-permute-done((bf16[1024,512]{1,0:T(8,128)(2,1)}, bf16[1024,512]{1,0:T(8,128)(2,1)S(1)}, u32[]{:S(2)}, u32[]{:S(2)}) %collective-permute-start) | collective-permute-done | bytes 1048608 | tf_op jit(solution)/shard_map/while/body/eval_jaxpr/ppermute | solution.py:51
  607.9 17.8 %collective-permute-done = bf16[1024,512]{1,0:T(8,128)(2,1)S(1)} collective-permute-done((bf16[1024,512]{1,0:T(8,128)(2,1)}, bf16[1024,512]{1,0:T(8,128)(2,1)S(1)}, u32[]{:S(2)}, u32[]{:S(2)}) %collective-permute-start) | collective-permute-done | bytes 1048608 | tf_op jit(solution)/shard_map/while/body/eval_jaxpr/ppermute | solution.py:51
  653.1 17.8 %collective-permute-done = bf16[1024,512]{1,0:T(8,128)(2,1)S(1)} collective-permute-done((bf16[1024,512]{1,0:T(8,128)(2,1)}, bf16[1024,512]{1,0:T(8,128)(2,1)S(1)}, u32[]{:S(2)}, u32[]{:S(2)}) %collective-permute-start) | collective-permute-done | bytes 1048608 | tf_op jit(solution)/shard_map/while/body/eval_jaxpr/ppermute | solution.py:51
  682.1 11.3 collective-permute-done.1
  698.2 17.8 %collective-permute-done = bf16[1024,512]{1,0:T(8,128)(2,1)S(1)} collective-permute-done((bf16[1024,512]{1,0:T(8,128)(2,1)}, bf16[1024,512]{1,0:T(8,128)(2,1)S(1)}, u32[]{:S(2)}, u32[]{:S(2)}) %collective-permute-start) | collective-permute-done | bytes 1048608 | tf_op jit(solution)/shard_map/while/body/eval_jaxpr/ppermute | solution.py:51
  727.2 11.3 collective-permute-done.1
  743.4 17.8 %collective-permute-done = bf16[1024,512]{1,0:T(8,128)(2,1)S(1)} collective-permute-done((bf16[1024,512]{1,0:T(8,128)(2,1)}, bf16[1024,512]{1,0:T(8,128)(2,1)S(1)}, u32[]{:S(2)}, u32[]{:S(2)}) %collective-permute-start) | collective-permute-done | bytes 1048608 | tf_op jit(solution)/shard_map/while/body/eval_jaxpr/ppermute | solution.py:51
  788.6 17.8 %collective-permute-done = bf16[1024,512]{1,0:T(8,128)(2,1)S(1)} collective-permute-done((bf16[1024,512]{1,0:T(8,128)(2,1)}, bf16[1024,512]{1,0:T(8,128)(2,1)S(1)}, u32[]{:S(2)}, u32[]{:S(2)}) %collective-permute-start) | collective-permute-done | bytes 1048608 | tf_op jit(solution)/shard_map/while/body/eval_jaxpr/ppermute | solution.py:51
  833.8 17.8 %collective-permute-done = bf16[1024,512]{1,0:T(8,128)(2,1)S(1)} collective-permute-done((bf16[1024,512]{1,0:T(8,128)(2,1)}, bf16[1024,512]{1,0:T(8,128)(2,1)S(1)}, u32[]{:S(2)}, u32[]{:S(2)}) %collective-permute-start) | collective-permute-done | bytes 1048608 | tf_op jit(solution)/shard_map/while/body/eval_jaxpr/ppermute | solution.py:51
  879.0 17.8 %collective-permute-done = bf16[1024,512]{1,0:T(8,128)(2,1)S(1)} collective-permute-done((bf16[1024,512]{1,0:T(8,128)(2,1)}, bf16[1024,512]{1,0:T(8,128)(2,1)S(1)}, u32[]{:S(2)}, u32[]{:S(2)}) %collective-permute-start) | collective-permute-done | bytes 1048608 | tf_op jit(solution)/shard_map/while/body/eval_jaxpr/ppermute | solution.py:51
  908.0 11.3 collective-permute-done.1
  924.2 17.8 %collective-permute-done = bf16[1024,512]{1,0:T(8,128)(2,1)S(1)} collective-permute-done((bf16[1024,512]{1,0:T(8,128)(2,1)}, bf16[1024,512]{1,0:T(8,128)(2,1)S(1)}, u32[]{:S(2)}, u32[]{:S(2)}) %collective-permute-start) | collective-permute-done | bytes 1048608 | tf_op jit(solution)/shard_map/while/body/eval_jaxpr/ppermute | solution.py:51
  953.1 11.3 collective-permute-done.1
  969.3 17.8 %collective-permute-done = bf16[1024,512]{1,0:T(8,128)(2,1)S(1)} collective-permute-done((bf16[1024,512]{1,0:T(8,128)(2,1)}, bf16[1024,512]{1,0:T(8,128)(2,1)S(1)}, u32[]{:S(2)}, u32[]{:S(2)}) %collective-permute-start) | collective-permute-done | bytes 1048608 | tf_op jit(solution)/shard_map/while/body/eval_jaxpr/ppermute | solution.py:51
  1014.5 17.8 %collective-permute-done = bf16[1024,512]{1,0:T(8,128)(2,1)S(1)} collective-permute-done((bf16[1024,512]{1,0:T(8,128)(2,1)}, bf16[1024,512]{1,0:T(8,128)(2,1)S(1)}, u32[]{:S(2)}, u32[]{:S(2)}) %collective-permute-start) | collective-permute-done | bytes 1048608 | tf_op jit(solution)/shard_map/while/body/eval_jaxpr/ppermute | solution.py:51
  1059.7 17.8 %collective-permute-done = bf16[1024,512]{1,0:T(8,128)(2,1)S(1)} collective-permute-done((bf16[1024,512]{1,0:T(8,128)(2,1)}, bf16[1024,512]{1,0:T(8,128)(2,1)S(1)}, u32[]{:S(2)}, u32[]{:S(2)}) %collective-permute-start) | collective-permute-done | bytes 1048608 | tf_op jit(solution)/shard_map/while/body/eval_jaxpr/ppermute | solution.py:51
  1104.9 17.8 %collective-permute-done = bf16[1024,512]{1,0:T(8,128)(2,1)S(1)} collective-permute-done((bf16[1024,512]{1,0:T(8,128)(2,1)}, bf16[1024,512]{1,0:T(8,128)(2,1)S(1)}, u32[]{:S(2)}, u32[]{:S(2)}) %collective-permute-start) | collective-permute-done | bytes 1048608 | tf_op jit(solution)/shard_map/while/body/eval_jaxpr/ppermute | solution.py:51
  1133.9 11.3 collective-permute-done.1
  1150.1 17.8 %collective-permute-done = bf16[1024,512]{1,0:T(8,128)(2,1)S(1)} collective-permute-done((bf16[1024,512]{1,0:T(8,128)(2,1)}, bf16[1024,512]{1,0:T(8,128)(2,1)S(1)}, u32[]{:S(2)}, u32[]{:S(2)}) %collective-permute-start) | collective-permute-done | bytes 1048608 | tf_op jit(solution)/shard_map/while/body/eval_jaxpr/ppermute | solution.py:51
  1179.0 11.3 collective-permute-done.1
  1195.2 17.8 %collective-permute-done = bf16[1024,512]{1,0:T(8,128)(2,1)S(1)} collective-permute-done((bf16[1024,512]{1,0:T(8,128)(2,1)}, bf16[1024,512]{1,0:T(8,128)(2,1)S(1)}, u32[]{:S(2)}, u32[]{:S(2)}) %collective-permute-start) | collective-permute-done | bytes 1048608 | tf_op jit(solution)/shard_map/while/body/eval_jaxpr/ppermute | solution.py:51
  1240.4 17.8 %collective-permute-done = bf16[1024,512]{1,0:T(8,128)(2,1)S(1)} collective-permute-done((bf16[1024,512]{1,0:T(8,128)(2,1)}, bf16[1024,512]{1,0:T(8,128)(2,1)S(1)}, u32[]{:S(2)}, u32[]{:S(2)}) %collective-permute-start) | collective-permute-done | bytes 1048608 | tf_op jit(solution)/shard_map/while/body/eval_jaxpr/ppermute | solution.py:51
  1285.6 17.8 %collective-permute-done = bf16[1024,512]{1,0:T(8,128)(2,1)S(1)} collective-permute-done((bf16[1024,512]{1,0:T(8,128)(2,1)}, bf16[1024,512]{1,0:T(8,128)(2,1)S(1)}, u32[]{:S(2)}, u32[]{:S(2)}) %collective-permute-start) | collective-permute-done | bytes 1048608 | tf_op jit(solution)/shard_map/while/body/eval_jaxpr/ppermute | solution.py:51
  1330.8 17.8 %collective-permute-done = bf16[1024,512]{1,0:T(8,128)(2,1)S(1)} collective-permute-done((bf16[1024,512]{1,0:T(8,128)(2,1)}, bf16[1024,512]{1,0:T(8,128)(2,1)S(1)}, u32[]{:S(2)}, u32[]{:S(2)}) %collective-permute-start) | collective-permute-done | bytes 1048608 | tf_op jit(solution)/shard_map/while/body/eval_jaxpr/ppermute | solution.py:51
  1359.8 11.3 collective-permute-done.1
  1376.0 17.8 %collective-permute-done = bf16[1024,512]{1,0:T(8,128)(2,1)S(1)} collective-permute-done((bf16[1024,512]{1,0:T(8,128)(2,1)}, bf16[1024,512]{1,0:T(8,128)(2,1)S(1)}, u32[]{:S(2)}, u32[]{:S(2)}) %collective-permute-start) | collective-permute-done | bytes 1048608 | tf_op jit(solution)/shard_map/while/body/eval_jaxpr/ppermute | solution.py:51
  1404.9 11.3 collective-permute-done.1
  1421.2 48.3 %psum.7 = f32[3]{0:T(128)S(1)} all-reduce(f32[3]{0:T(128)S(1)} %get-tuple-element.49), channel_id=1, replica_groups=mesh['dp'=32] {'dp'}, use_global_device_ids=true, to_apply=%region_10.11 | all-reduce | flops 3 | bytes 24 | tf_op jit(solution)/shard_map/psum | solution.py:59
  (394 shorter events, 709.0 us)
Async XLA Ops:
  19.4 18.9 %collective-permute-start = (bf16[1024,512]{1,0:T(8,128)(2,1)}, bf16[1024,512]{1,0:T(8,128)(2,1)S(1)}, u32[]{:S(2)}, u32[]{:S(2)}) collective-permute-start(bf16[1024,512]{1,0:T(8,128)(2,1)} %get-tuple-element.152), channel_id=1, source_target_pairs={{0,1},{1,2},{2,3},{3,4},{4,5},{5,6},{6,7},{7,8},{8,9},{9,10},{10,1... | collective-permute-start | bytes 3145736 | tf_op jit(solution)/shard_map/while/body/eval_jaxpr/ppermute | solution.py:51
  19.9 40.9 %collective-permute-start.1 = (f32[1024,512]{1,0:T(8,128)}, f32[1024,512]{1,0:T(8,128)}, u32[]{:S(2)}, u32[]{:S(2)}) collective-permute-start(f32[1024,512]{1,0:T(8,128)} %get-tuple-element.153), channel_id=1, source_target_pairs={{0,1},{1,2},{2,3},{3,4},{4,5},{5,6},{6,7},{7,8},{8,9},{9,10},{10,1... | collective-permute-start | bytes 6291464 | tf_op jit(solution)/shard_map/while/body/eval_jaxpr/ppermute | solution.py:52
  65.7 17.8 %collective-permute-start = (bf16[1024,512]{1,0:T(8,128)(2,1)}, bf16[1024,512]{1,0:T(8,128)(2,1)S(1)}, u32[]{:S(2)}, u32[]{:S(2)}) collective-permute-start(bf16[1024,512]{1,0:T(8,128)(2,1)} %get-tuple-element.152), channel_id=1, source_target_pairs={{0,1},{1,2},{2,3},{3,4},{4,5},{5,6},{6,7},{7,8},{8,9},{9,10},{10,1... | collective-permute-start | bytes 3145736 | tf_op jit(solution)/shard_map/while/body/eval_jaxpr/ppermute | solution.py:51
  65.7 40.3 %collective-permute-start.1 = (f32[1024,512]{1,0:T(8,128)}, f32[1024,512]{1,0:T(8,128)}, u32[]{:S(2)}, u32[]{:S(2)}) collective-permute-start(f32[1024,512]{1,0:T(8,128)} %get-tuple-element.153), channel_id=1, source_target_pairs={{0,1},{1,2},{2,3},{3,4},{4,5},{5,6},{6,7},{7,8},{8,9},{9,10},{10,1... | collective-permute-start | bytes 6291464 | tf_op jit(solution)/shard_map/while/body/eval_jaxpr/ppermute | solution.py:52
  110.9 17.8 %collective-permute-start = (bf16[1024,512]{1,0:T(8,128)(2,1)}, bf16[1024,512]{1,0:T(8,128)(2,1)S(1)}, u32[]{:S(2)}, u32[]{:S(2)}) collective-permute-start(bf16[1024,512]{1,0:T(8,128)(2,1)} %get-tuple-element.152), channel_id=1, source_target_pairs={{0,1},{1,2},{2,3},{3,4},{4,5},{5,6},{6,7},{7,8},{8,9},{9,10},{10,1... | collective-permute-start | bytes 3145736 | tf_op jit(solution)/shard_map/while/body/eval_jaxpr/ppermute | solution.py:51
  110.9 40.3 %collective-permute-start.1 = (f32[1024,512]{1,0:T(8,128)}, f32[1024,512]{1,0:T(8,128)}, u32[]{:S(2)}, u32[]{:S(2)}) collective-permute-start(f32[1024,512]{1,0:T(8,128)} %get-tuple-element.153), channel_id=1, source_target_pairs={{0,1},{1,2},{2,3},{3,4},{4,5},{5,6},{6,7},{7,8},{8,9},{9,10},{10,1... | collective-permute-start | bytes 6291464 | tf_op jit(solution)/shard_map/while/body/eval_jaxpr/ppermute | solution.py:52
  156.1 17.8 %collective-permute-start = (bf16[1024,512]{1,0:T(8,128)(2,1)}, bf16[1024,512]{1,0:T(8,128)(2,1)S(1)}, u32[]{:S(2)}, u32[]{:S(2)}) collective-permute-start(bf16[1024,512]{1,0:T(8,128)(2,1)} %get-tuple-element.152), channel_id=1, source_target_pairs={{0,1},{1,2},{2,3},{3,4},{4,5},{5,6},{6,7},{7,8},{8,9},{9,10},{10,1... | collective-permute-start | bytes 3145736 | tf_op jit(solution)/shard_map/while/body/eval_jaxpr/ppermute | solution.py:51
  156.1 40.3 %collective-permute-start.1 = (f32[1024,512]{1,0:T(8,128)}, f32[1024,512]{1,0:T(8,128)}, u32[]{:S(2)}, u32[]{:S(2)}) collective-permute-start(f32[1024,512]{1,0:T(8,128)} %get-tuple-element.153), channel_id=1, source_target_pairs={{0,1},{1,2},{2,3},{3,4},{4,5},{5,6},{6,7},{7,8},{8,9},{9,10},{10,1... | collective-permute-start | bytes 6291464 | tf_op jit(solution)/shard_map/while/body/eval_jaxpr/ppermute | solution.py:52
  201.2 17.8 %collective-permute-start = (bf16[1024,512]{1,0:T(8,128)(2,1)}, bf16[1024,512]{1,0:T(8,128)(2,1)S(1)}, u32[]{:S(2)}, u32[]{:S(2)}) collective-permute-start(bf16[1024,512]{1,0:T(8,128)(2,1)} %get-tuple-element.152), channel_id=1, source_target_pairs={{0,1},{1,2},{2,3},{3,4},{4,5},{5,6},{6,7},{7,8},{8,9},{9,10},{10,1... | collective-permute-start | bytes 3145736 | tf_op jit(solution)/shard_map/while/body/eval_jaxpr/ppermute | solution.py:51
  201.3 40.3 %collective-permute-start.1 = (f32[1024,512]{1,0:T(8,128)}, f32[1024,512]{1,0:T(8,128)}, u32[]{:S(2)}, u32[]{:S(2)}) collective-permute-start(f32[1024,512]{1,0:T(8,128)} %get-tuple-element.153), channel_id=1, source_target_pairs={{0,1},{1,2},{2,3},{3,4},{4,5},{5,6},{6,7},{7,8},{8,9},{9,10},{10,1... | collective-permute-start | bytes 6291464 | tf_op jit(solution)/shard_map/while/body/eval_jaxpr/ppermute | solution.py:52
  246.4 17.8 %collective-permute-start = (bf16[1024,512]{1,0:T(8,128)(2,1)}, bf16[1024,512]{1,0:T(8,128)(2,1)S(1)}, u32[]{:S(2)}, u32[]{:S(2)}) collective-permute-start(bf16[1024,512]{1,0:T(8,128)(2,1)} %get-tuple-element.152), channel_id=1, source_target_pairs={{0,1},{1,2},{2,3},{3,4},{4,5},{5,6},{6,7},{7,8},{8,9},{9,10},{10,1... | collective-permute-start | bytes 3145736 | tf_op jit(solution)/shard_map/while/body/eval_jaxpr/ppermute | solution.py:51
  246.4 40.3 %collective-permute-start.1 = (f32[1024,512]{1,0:T(8,128)}, f32[1024,512]{1,0:T(8,128)}, u32[]{:S(2)}, u32[]{:S(2)}) collective-permute-start(f32[1024,512]{1,0:T(8,128)} %get-tuple-element.153), channel_id=1, source_target_pairs={{0,1},{1,2},{2,3},{3,4},{4,5},{5,6},{6,7},{7,8},{8,9},{9,10},{10,1... | collective-permute-start | bytes 6291464 | tf_op jit(solution)/shard_map/while/body/eval_jaxpr/ppermute | solution.py:52
  291.6 17.8 %collective-permute-start = (bf16[1024,512]{1,0:T(8,128)(2,1)}, bf16[1024,512]{1,0:T(8,128)(2,1)S(1)}, u32[]{:S(2)}, u32[]{:S(2)}) collective-permute-start(bf16[1024,512]{1,0:T(8,128)(2,1)} %get-tuple-element.152), channel_id=1, source_target_pairs={{0,1},{1,2},{2,3},{3,4},{4,5},{5,6},{6,7},{7,8},{8,9},{9,10},{10,1... | collective-permute-start | bytes 3145736 | tf_op jit(solution)/shard_map/while/body/eval_jaxpr/ppermute | solution.py:51
  291.6 40.3 %collective-permute-start.1 = (f32[1024,512]{1,0:T(8,128)}, f32[1024,512]{1,0:T(8,128)}, u32[]{:S(2)}, u32[]{:S(2)}) collective-permute-start(f32[1024,512]{1,0:T(8,128)} %get-tuple-element.153), channel_id=1, source_target_pairs={{0,1},{1,2},{2,3},{3,4},{4,5},{5,6},{6,7},{7,8},{8,9},{9,10},{10,1... | collective-permute-start | bytes 6291464 | tf_op jit(solution)/shard_map/while/body/eval_jaxpr/ppermute | solution.py:52
  336.8 17.8 %collective-permute-start = (bf16[1024,512]{1,0:T(8,128)(2,1)}, bf16[1024,512]{1,0:T(8,128)(2,1)S(1)}, u32[]{:S(2)}, u32[]{:S(2)}) collective-permute-start(bf16[1024,512]{1,0:T(8,128)(2,1)} %get-tuple-element.152), channel_id=1, source_target_pairs={{0,1},{1,2},{2,3},{3,4},{4,5},{5,6},{6,7},{7,8},{8,9},{9,10},{10,1... | collective-permute-start | bytes 3145736 | tf_op jit(solution)/shard_map/while/body/eval_jaxpr/ppermute | solution.py:51
  336.8 40.3 %collective-permute-start.1 = (f32[1024,512]{1,0:T(8,128)}, f32[1024,512]{1,0:T(8,128)}, u32[]{:S(2)}, u32[]{:S(2)}) collective-permute-start(f32[1024,512]{1,0:T(8,128)} %get-tuple-element.153), channel_id=1, source_target_pairs={{0,1},{1,2},{2,3},{3,4},{4,5},{5,6},{6,7},{7,8},{8,9},{9,10},{10,1... | collective-permute-start | bytes 6291464 | tf_op jit(solution)/shard_map/while/body/eval_jaxpr/ppermute | solution.py:52
  382.0 17.8 %collective-permute-start = (bf16[1024,512]{1,0:T(8,128)(2,1)}, bf16[1024,512]{1,0:T(8,128)(2,1)S(1)}, u32[]{:S(2)}, u32[]{:S(2)}) collective-permute-start(bf16[1024,512]{1,0:T(8,128)(2,1)} %get-tuple-element.152), channel_id=1, source_target_pairs={{0,1},{1,2},{2,3},{3,4},{4,5},{5,6},{6,7},{7,8},{8,9},{9,10},{10,1... | collective-permute-start | bytes 3145736 | tf_op jit(solution)/shard_map/while/body/eval_jaxpr/ppermute | solution.py:51
  382.0 40.3 %collective-permute-start.1 = (f32[1024,512]{1,0:T(8,128)}, f32[1024,512]{1,0:T(8,128)}, u32[]{:S(2)}, u32[]{:S(2)}) collective-permute-start(f32[1024,512]{1,0:T(8,128)} %get-tuple-element.153), channel_id=1, source_target_pairs={{0,1},{1,2},{2,3},{3,4},{4,5},{5,6},{6,7},{7,8},{8,9},{9,10},{10,1... | collective-permute-start | bytes 6291464 | tf_op jit(solution)/shard_map/while/body/eval_jaxpr/ppermute | solution.py:52
  427.2 17.8 %collective-permute-start = (bf16[1024,512]{1,0:T(8,128)(2,1)}, bf16[1024,512]{1,0:T(8,128)(2,1)S(1)}, u32[]{:S(2)}, u32[]{:S(2)}) collective-permute-start(bf16[1024,512]{1,0:T(8,128)(2,1)} %get-tuple-element.152), channel_id=1, source_target_pairs={{0,1},{1,2},{2,3},{3,4},{4,5},{5,6},{6,7},{7,8},{8,9},{9,10},{10,1... | collective-permute-start | bytes 3145736 | tf_op jit(solution)/shard_map/while/body/eval_jaxpr/ppermute | solution.py:51
  427.2 40.3 %collective-permute-start.1 = (f32[1024,512]{1,0:T(8,128)}, f32[1024,512]{1,0:T(8,128)}, u32[]{:S(2)}, u32[]{:S(2)}) collective-permute-start(f32[1024,512]{1,0:T(8,128)} %get-tuple-element.153), channel_id=1, source_target_pairs={{0,1},{1,2},{2,3},{3,4},{4,5},{5,6},{6,7},{7,8},{8,9},{9,10},{10,1... | collective-permute-start | bytes 6291464 | tf_op jit(solution)/shard_map/while/body/eval_jaxpr/ppermute | solution.py:52
  472.3 17.8 %collective-permute-start = (bf16[1024,512]{1,0:T(8,128)(2,1)}, bf16[1024,512]{1,0:T(8,128)(2,1)S(1)}, u32[]{:S(2)}, u32[]{:S(2)}) collective-permute-start(bf16[1024,512]{1,0:T(8,128)(2,1)} %get-tuple-element.152), channel_id=1, source_target_pairs={{0,1},{1,2},{2,3},{3,4},{4,5},{5,6},{6,7},{7,8},{8,9},{9,10},{10,1... | collective-permute-start | bytes 3145736 | tf_op jit(solution)/shard_map/while/body/eval_jaxpr/ppermute | solution.py:51
  472.3 40.3 %collective-permute-start.1 = (f32[1024,512]{1,0:T(8,128)}, f32[1024,512]{1,0:T(8,128)}, u32[]{:S(2)}, u32[]{:S(2)}) collective-permute-start(f32[1024,512]{1,0:T(8,128)} %get-tuple-element.153), channel_id=1, source_target_pairs={{0,1},{1,2},{2,3},{3,4},{4,5},{5,6},{6,7},{7,8},{8,9},{9,10},{10,1... | collective-permute-start | bytes 6291464 | tf_op jit(solution)/shard_map/while/body/eval_jaxpr/ppermute | solution.py:52
  517.5 17.8 %collective-permute-start = (bf16[1024,512]{1,0:T(8,128)(2,1)}, bf16[1024,512]{1,0:T(8,128)(2,1)S(1)}, u32[]{:S(2)}, u32[]{:S(2)}) collective-permute-start(bf16[1024,512]{1,0:T(8,128)(2,1)} %get-tuple-element.152), channel_id=1, source_target_pairs={{0,1},{1,2},{2,3},{3,4},{4,5},{5,6},{6,7},{7,8},{8,9},{9,10},{10,1... | collective-permute-start | bytes 3145736 | tf_op jit(solution)/shard_map/while/body/eval_jaxpr/ppermute | solution.py:51
  517.5 40.3 %collective-permute-start.1 = (f32[1024,512]{1,0:T(8,128)}, f32[1024,512]{1,0:T(8,128)}, u32[]{:S(2)}, u32[]{:S(2)}) collective-permute-start(f32[1024,512]{1,0:T(8,128)} %get-tuple-element.153), channel_id=1, source_target_pairs={{0,1},{1,2},{2,3},{3,4},{4,5},{5,6},{6,7},{7,8},{8,9},{9,10},{10,1... | collective-permute-start | bytes 6291464 | tf_op jit(solution)/shard_map/while/body/eval_jaxpr/ppermute | solution.py:52
  562.7 17.8 %collective-permute-start = (bf16[1024,512]{1,0:T(8,128)(2,1)}, bf16[1024,512]{1,0:T(8,128)(2,1)S(1)}, u32[]{:S(2)}, u32[]{:S(2)}) collective-permute-start(bf16[1024,512]{1,0:T(8,128)(2,1)} %get-tuple-element.152), channel_id=1, source_target_pairs={{0,1},{1,2},{2,3},{3,4},{4,5},{5,6},{6,7},{7,8},{8,9},{9,10},{10,1... | collective-permute-start | bytes 3145736 | tf_op jit(solution)/shard_map/while/body/eval_jaxpr/ppermute | solution.py:51
  562.7 40.3 %collective-permute-start.1 = (f32[1024,512]{1,0:T(8,128)}, f32[1024,512]{1,0:T(8,128)}, u32[]{:S(2)}, u32[]{:S(2)}) collective-permute-start(f32[1024,512]{1,0:T(8,128)} %get-tuple-element.153), channel_id=1, source_target_pairs={{0,1},{1,2},{2,3},{3,4},{4,5},{5,6},{6,7},{7,8},{8,9},{9,10},{10,1... | collective-permute-start | bytes 6291464 | tf_op jit(solution)/shard_map/while/body/eval_jaxpr/ppermute | solution.py:52
  607.9 17.8 %collective-permute-start = (bf16[1024,512]{1,0:T(8,128)(2,1)}, bf16[1024,512]{1,0:T(8,128)(2,1)S(1)}, u32[]{:S(2)}, u32[]{:S(2)}) collective-permute-start(bf16[1024,512]{1,0:T(8,128)(2,1)} %get-tuple-element.152), channel_id=1, source_target_pairs={{0,1},{1,2},{2,3},{3,4},{4,5},{5,6},{6,7},{7,8},{8,9},{9,10},{10,1... | collective-permute-start | bytes 3145736 | tf_op jit(solution)/shard_map/while/body/eval_jaxpr/ppermute | solution.py:51
  607.9 40.3 %collective-permute-start.1 = (f32[1024,512]{1,0:T(8,128)}, f32[1024,512]{1,0:T(8,128)}, u32[]{:S(2)}, u32[]{:S(2)}) collective-permute-start(f32[1024,512]{1,0:T(8,128)} %get-tuple-element.153), channel_id=1, source_target_pairs={{0,1},{1,2},{2,3},{3,4},{4,5},{5,6},{6,7},{7,8},{8,9},{9,10},{10,1... | collective-permute-start | bytes 6291464 | tf_op jit(solution)/shard_map/while/body/eval_jaxpr/ppermute | solution.py:52
  653.1 17.8 %collective-permute-start = (bf16[1024,512]{1,0:T(8,128)(2,1)}, bf16[1024,512]{1,0:T(8,128)(2,1)S(1)}, u32[]{:S(2)}, u32[]{:S(2)}) collective-permute-start(bf16[1024,512]{1,0:T(8,128)(2,1)} %get-tuple-element.152), channel_id=1, source_target_pairs={{0,1},{1,2},{2,3},{3,4},{4,5},{5,6},{6,7},{7,8},{8,9},{9,10},{10,1... | collective-permute-start | bytes 3145736 | tf_op jit(solution)/shard_map/while/body/eval_jaxpr/ppermute | solution.py:51
  653.1 40.3 %collective-permute-start.1 = (f32[1024,512]{1,0:T(8,128)}, f32[1024,512]{1,0:T(8,128)}, u32[]{:S(2)}, u32[]{:S(2)}) collective-permute-start(f32[1024,512]{1,0:T(8,128)} %get-tuple-element.153), channel_id=1, source_target_pairs={{0,1},{1,2},{2,3},{3,4},{4,5},{5,6},{6,7},{7,8},{8,9},{9,10},{10,1... | collective-permute-start | bytes 6291464 | tf_op jit(solution)/shard_map/while/body/eval_jaxpr/ppermute | solution.py:52
  698.2 17.8 %collective-permute-start = (bf16[1024,512]{1,0:T(8,128)(2,1)}, bf16[1024,512]{1,0:T(8,128)(2,1)S(1)}, u32[]{:S(2)}, u32[]{:S(2)}) collective-permute-start(bf16[1024,512]{1,0:T(8,128)(2,1)} %get-tuple-element.152), channel_id=1, source_target_pairs={{0,1},{1,2},{2,3},{3,4},{4,5},{5,6},{6,7},{7,8},{8,9},{9,10},{10,1... | collective-permute-start | bytes 3145736 | tf_op jit(solution)/shard_map/while/body/eval_jaxpr/ppermute | solution.py:51
  698.2 40.3 %collective-permute-start.1 = (f32[1024,512]{1,0:T(8,128)}, f32[1024,512]{1,0:T(8,128)}, u32[]{:S(2)}, u32[]{:S(2)}) collective-permute-start(f32[1024,512]{1,0:T(8,128)} %get-tuple-element.153), channel_id=1, source_target_pairs={{0,1},{1,2},{2,3},{3,4},{4,5},{5,6},{6,7},{7,8},{8,9},{9,10},{10,1... | collective-permute-start | bytes 6291464 | tf_op jit(solution)/shard_map/while/body/eval_jaxpr/ppermute | solution.py:52
  743.4 40.3 %collective-permute-start.1 = (f32[1024,512]{1,0:T(8,128)}, f32[1024,512]{1,0:T(8,128)}, u32[]{:S(2)}, u32[]{:S(2)}) collective-permute-start(f32[1024,512]{1,0:T(8,128)} %get-tuple-element.153), channel_id=1, source_target_pairs={{0,1},{1,2},{2,3},{3,4},{4,5},{5,6},{6,7},{7,8},{8,9},{9,10},{10,1... | collective-permute-start | bytes 6291464 | tf_op jit(solution)/shard_map/while/body/eval_jaxpr/ppermute | solution.py:52
  788.6 40.3 %collective-permute-start.1 = (f32[1024,512]{1,0:T(8,128)}, f32[1024,512]{1,0:T(8,128)}, u32[]{:S(2)}, u32[]{:S(2)}) collective-permute-start(f32[1024,512]{1,0:T(8,128)} %get-tuple-element.153), channel_id=1, source_target_pairs={{0,1},{1,2},{2,3},{3,4},{4,5},{5,6},{6,7},{7,8},{8,9},{9,10},{10,1... | collective-permute-start | bytes 6291464 | tf_op jit(solution)/shard_map/while/body/eval_jaxpr/ppermute | solution.py:52
  833.8 40.3 %collective-permute-start.1 = (f32[1024,512]{1,0:T(8,128)}, f32[1024,512]{1,0:T(8,128)}, u32[]{:S(2)}, u32[]{:S(2)}) collective-permute-start(f32[1024,512]{1,0:T(8,128)} %get-tuple-element.153), channel_id=1, source_target_pairs={{0,1},{1,2},{2,3},{3,4},{4,5},{5,6},{6,7},{7,8},{8,9},{9,10},{10,1... | collective-permute-start | bytes 6291464 | tf_op jit(solution)/shard_map/while/body/eval_jaxpr/ppermute | solution.py:52
  879.0 40.3 %collective-permute-start.1 = (f32[1024,512]{1,0:T(8,128)}, f32[1024,512]{1,0:T(8,128)}, u32[]{:S(2)}, u32[]{:S(2)}) collective-permute-start(f32[1024,512]{1,0:T(8,128)} %get-tuple-element.153), channel_id=1, source_target_pairs={{0,1},{1,2},{2,3},{3,4},{4,5},{5,6},{6,7},{7,8},{8,9},{9,10},{10,1... | collective-permute-start | bytes 6291464 | tf_op jit(solution)/shard_map/while/body/eval_jaxpr/ppermute | solution.py:52
  924.1 40.3 %collective-permute-start.1 = (f32[1024,512]{1,0:T(8,128)}, f32[1024,512]{1,0:T(8,128)}, u32[]{:S(2)}, u32[]{:S(2)}) collective-permute-start(f32[1024,512]{1,0:T(8,128)} %get-tuple-element.153), channel_id=1, source_target_pairs={{0,1},{1,2},{2,3},{3,4},{4,5},{5,6},{6,7},{7,8},{8,9},{9,10},{10,1... | collective-permute-start | bytes 6291464 | tf_op jit(solution)/shard_map/while/body/eval_jaxpr/ppermute | solution.py:52
  969.3 40.3 %collective-permute-start.1 = (f32[1024,512]{1,0:T(8,128)}, f32[1024,512]{1,0:T(8,128)}, u32[]{:S(2)}, u32[]{:S(2)}) collective-permute-start(f32[1024,512]{1,0:T(8,128)} %get-tuple-element.153), channel_id=1, source_target_pairs={{0,1},{1,2},{2,3},{3,4},{4,5},{5,6},{6,7},{7,8},{8,9},{9,10},{10,1... | collective-permute-start | bytes 6291464 | tf_op jit(solution)/shard_map/while/body/eval_jaxpr/ppermute | solution.py:52
  1014.5 40.3 %collective-permute-start.1 = (f32[1024,512]{1,0:T(8,128)}, f32[1024,512]{1,0:T(8,128)}, u32[]{:S(2)}, u32[]{:S(2)}) collective-permute-start(f32[1024,512]{1,0:T(8,128)} %get-tuple-element.153), channel_id=1, source_target_pairs={{0,1},{1,2},{2,3},{3,4},{4,5},{5,6},{6,7},{7,8},{8,9},{9,10},{10,1... | collective-permute-start | bytes 6291464 | tf_op jit(solution)/shard_map/while/body/eval_jaxpr/ppermute | solution.py:52
  1059.7 40.3 %collective-permute-start.1 = (f32[1024,512]{1,0:T(8,128)}, f32[1024,512]{1,0:T(8,128)}, u32[]{:S(2)}, u32[]{:S(2)}) collective-permute-start(f32[1024,512]{1,0:T(8,128)} %get-tuple-element.153), channel_id=1, source_target_pairs={{0,1},{1,2},{2,3},{3,4},{4,5},{5,6},{6,7},{7,8},{8,9},{9,10},{10,1... | collective-permute-start | bytes 6291464 | tf_op jit(solution)/shard_map/while/body/eval_jaxpr/ppermute | solution.py:52
  1104.9 40.3 %collective-permute-start.1 = (f32[1024,512]{1,0:T(8,128)}, f32[1024,512]{1,0:T(8,128)}, u32[]{:S(2)}, u32[]{:S(2)}) collective-permute-start(f32[1024,512]{1,0:T(8,128)} %get-tuple-element.153), channel_id=1, source_target_pairs={{0,1},{1,2},{2,3},{3,4},{4,5},{5,6},{6,7},{7,8},{8,9},{9,10},{10,1... | collective-permute-start | bytes 6291464 | tf_op jit(solution)/shard_map/while/body/eval_jaxpr/ppermute | solution.py:52
  1150.0 40.3 %collective-permute-start.1 = (f32[1024,512]{1,0:T(8,128)}, f32[1024,512]{1,0:T(8,128)}, u32[]{:S(2)}, u32[]{:S(2)}) collective-permute-start(f32[1024,512]{1,0:T(8,128)} %get-tuple-element.153), channel_id=1, source_target_pairs={{0,1},{1,2},{2,3},{3,4},{4,5},{5,6},{6,7},{7,8},{8,9},{9,10},{10,1... | collective-permute-start | bytes 6291464 | tf_op jit(solution)/shard_map/while/body/eval_jaxpr/ppermute | solution.py:52
  1195.2 40.3 %collective-permute-start.1 = (f32[1024,512]{1,0:T(8,128)}, f32[1024,512]{1,0:T(8,128)}, u32[]{:S(2)}, u32[]{:S(2)}) collective-permute-start(f32[1024,512]{1,0:T(8,128)} %get-tuple-element.153), channel_id=1, source_target_pairs={{0,1},{1,2},{2,3},{3,4},{4,5},{5,6},{6,7},{7,8},{8,9},{9,10},{10,1... | collective-permute-start | bytes 6291464 | tf_op jit(solution)/shard_map/while/body/eval_jaxpr/ppermute | solution.py:52
  1240.4 40.3 %collective-permute-start.1 = (f32[1024,512]{1,0:T(8,128)}, f32[1024,512]{1,0:T(8,128)}, u32[]{:S(2)}, u32[]{:S(2)}) collective-permute-start(f32[1024,512]{1,0:T(8,128)} %get-tuple-element.153), channel_id=1, source_target_pairs={{0,1},{1,2},{2,3},{3,4},{4,5},{5,6},{6,7},{7,8},{8,9},{9,10},{10,1... | collective-permute-start | bytes 6291464 | tf_op jit(solution)/shard_map/while/body/eval_jaxpr/ppermute | solution.py:52
  1285.6 40.3 %collective-permute-start.1 = (f32[1024,512]{1,0:T(8,128)}, f32[1024,512]{1,0:T(8,128)}, u32[]{:S(2)}, u32[]{:S(2)}) collective-permute-start(f32[1024,512]{1,0:T(8,128)} %get-tuple-element.153), channel_id=1, source_target_pairs={{0,1},{1,2},{2,3},{3,4},{4,5},{5,6},{6,7},{7,8},{8,9},{9,10},{10,1... | collective-permute-start | bytes 6291464 | tf_op jit(solution)/shard_map/while/body/eval_jaxpr/ppermute | solution.py:52
  1330.8 40.3 %collective-permute-start.1 = (f32[1024,512]{1,0:T(8,128)}, f32[1024,512]{1,0:T(8,128)}, u32[]{:S(2)}, u32[]{:S(2)}) collective-permute-start(f32[1024,512]{1,0:T(8,128)} %get-tuple-element.153), channel_id=1, source_target_pairs={{0,1},{1,2},{2,3},{3,4},{4,5},{5,6},{6,7},{7,8},{8,9},{9,10},{10,1... | collective-permute-start | bytes 6291464 | tf_op jit(solution)/shard_map/while/body/eval_jaxpr/ppermute | solution.py:52
  1375.9 40.3 %collective-permute-start.1 = (f32[1024,512]{1,0:T(8,128)}, f32[1024,512]{1,0:T(8,128)}, u32[]{:S(2)}, u32[]{:S(2)}) collective-permute-start(f32[1024,512]{1,0:T(8,128)} %get-tuple-element.153), channel_id=1, source_target_pairs={{0,1},{1,2},{2,3},{3,4},{4,5},{5,6},{6,7},{7,8},{8,9},{9,10},{10,1... | collective-permute-start | bytes 6291464 | tf_op jit(solution)/shard_map/while/body/eval_jaxpr/ppermute | solution.py:52
  1421.2 53.5 %collective-permute-start.2 = (f32[1024,512]{1,0:T(8,128)}, f32[1024,512]{1,0:T(8,128)}, u32[]{:S(2)}, u32[]{:S(2)}) collective-permute-start(f32[1024,512]{1,0:T(8,128)} %get-tuple-element.51), channel_id=1, source_target_pairs={{0,1},{1,2},{2,3},{3,4},{4,5},{5,6},{6,7},{7,8},{8,9},{9,10},{10,1... | collective-permute-start | bytes 6291464 | tf_op jit(solution)/shard_map/ppermute | solution.py:57
  (87 other events, 4000.9 us)
where the time goes:
time: 1480 us
  waiting for transfers between devices  900 us (61%)
  matrix products  418 us (28%)
  other arithmetic  75.6 us (5%)
  blocking collectives  48.3 us (3%)
  local copies, waits for them, and re-layouts  31.5 us (2%)
    ppermute x31, waiting for transfers between devices, visit_step(): txt_blk = lax.ppermute(txt_blk, 'dp', shift_pairs)  550 us
    ppermute x31, waiting for transfers between devices, visit_step(): txt_acc = lax.ppermute(txt_acc, 'dp', shift_pairs)  350 us
    dot_general x32, matrix products, pair_terms(): jnp.einsum('id,jd->ij', img_b, txt_blk, preferred_element_type=jnp.float32)  199 us
    dot_general x32, matrix products, pair_terms(): jnp.einsum('ij,id->jd', weights_b, img_b, preferred_element_type=jnp.floa...  154 us
    dot_general x32, matrix products, pair_terms(): jnp.einsum('ij,jd->id', weights_b, txt_blk, preferred_element_type=jnp.fl...  65.2 us
    add x31, other arithmetic, visit_step(): stat_sums + new_sums  60.4 us
    psum x1, blocking collectives, local_fn(): stat_sums = lax.psum(loop_state[3], 'dp') / total_rows  48.3 us
    while x155, local copies, waits for them, and re-layouts  30.8 us
  transfers between devices with their start and end apart: 63, of which 62 were waited for; matrix products, arithmetic and copies ran while one was open for 24% of the time, Pallas kernels for 0%

commit v1 on v0

v1 whole, which is shorter than its diff:
```python
import functools

import jax
import jax.numpy as jnp
from jax import lax
from jax.experimental import pallas as pl
from jax.experimental.pallas import tpu as pltpu
from jax.sharding import PartitionSpec as P

LOG2E = 1.4426950408889634
LN2 = 0.6931471805599453
NT_DIMS = (((1,), (1,)), ((), ()))
TN_DIMS = (((0,), (0,)), ((), ()))
ROWS = 1024
HALF = 512
WIDTH = 512

PARTS = 2
TASKS = (0, 8, 4, 12, 36, 32, 37, 9, 13, 24, 48, 53, 52, 33, 50, 49, 38, 29, 54, 21, 19, 51, 3, 23, 55, 31, 11, 43, 39, 61, 40, 59, 60, 57, 15, 7, 34, 63, 56, 58, 62, 47, 27, 35, 28, 44, 46, 1, 41, 42, 25, 45, 14, 26, 5, 30, 6, 10, 22, 17, 18, 2, 20, 16)
EVENTS = (
    (3, 'ty', 0),
    (3, 'iz', 0),
    (3, 'tz', 0),
    (3, 'ty', 1),
    (9, 'tyz', 0),
    (13, 'iz', 1),
    (13, 'tz', 1),
    (19, 'tyz', 1),
    (25, 'ux', 3, 0, 0),
    (25, 'ux', 3, 0, 1),
    (41, 'ux', 3, 1, 0),
    (41, 'ux', 3, 1, 1),
    (42, 'vc', 3),
    (44, 'uz', 0, 0),
    (44, 'uz', 0, 1),
    (44, 'vy', 3, 0, 0),
    (44, 'vy', 3, 0, 1),
    (44, 'vy', 3, 1, 0),
    (44, 'vy', 3, 1, 1),
    (52, 'uz', 1, 0),
    (52, 'uz', 1, 1),
    (55, 'vc', 1),
    (56, 'ux', 1, 1, 0),
    (56, 'ux', 1, 1, 1),
    (59, 'vc', 2),
    (60, 'vy', 1, 0, 0),
    (60, 'vy', 1, 0, 1),
    (60, 'vy', 1, 1, 0),
    (60, 'vy', 1, 1, 1),
    (62, 'vz', 0, 0),
    (62, 'vz', 0, 1),
    (62, 'vz', 1, 0),
    (62, 'vz', 1, 1),
    (63, 'vc', 0),
    (64, 'ux', 1, 0, 0),
    (64, 'ux', 1, 0, 1),
)
PIECE = HALF // PARTS
COPIES = {}


def _register():
    names = []
    for h in range(2):
        names += [("ix", h), ("iz", h), ("ixz", h), ("ty", h), ("tz", h), ("tyz", h)]
        names += [("tc", q, h) for q in range(4)]
        for p in range(PARTS):
            names += [("ux", 1, h, p), ("ux", 3, h, p), ("uz", h, p)]
            names += [("vy", 1, h, p), ("vy", 3, h, p), ("vz", h, p)]
    names += [("vc", q) for q in range(4)]
    names += [("st", k) for k in range(5)]
    for k, n in enumerate(names):
        COPIES[n] = k


_register()


def flip(me, bit):
    return me + bit - 2 * bit * lax.rem(lax.div(me, bit), 2)


def task_at(t):
    per = 5
    words = []
    for k in range(0, len(TASKS), per):
        word = 0
        for pos, code in enumerate(TASKS[k:k + per]):
            word |= code << (6 * pos)
        words.append(word)
    which, pos = lax.div(t, per), lax.rem(t, per)
    word = jnp.int32(words[0])
    for k in range(1, len(words)):
        word = jnp.where(which == k, jnp.int32(words[k]), word)
    code = jnp.int32(0)
    for k in range(per):
        code = jnp.where(pos == k, lax.rem(lax.div(word, jnp.int32(64 ** k)), 64), code)
    return lax.div(code, 8), lax.rem(code, 8)


def pair_kernel(sc_ref, xin, yin, u_out, v_out, st_out,
                X, Y, U, V, RX, RZ, RC, RY, RZ2, S, sums, ST, RS, send, recv, local):
    me = lax.axis_index("dp")
    core, xn, yn, z1, z2 = peers = [flip(me, b) for b in (1, 2, 4, 8, 16)]
    ts2, b2 = sc_ref[0], sc_ref[1]

    barrier = pltpu.get_barrier_semaphore()
    loads = [pltpu.make_async_copy(xin, X.at[pl.ds(0, ROWS)], local.at[0]),
             pltpu.make_async_copy(yin, Y.at[pl.ds(0, ROWS)], local.at[1])]
    for load in loads:
        load.start()
    for peer in peers:
        pl.semaphore_signal(barrier, inc=1, device_id=(peer,), device_id_type=pl.DeviceIdType.MESH)
    pl.semaphore_wait(barrier, 5)
    for load in loads:
        load.wait()

    def rows(block, h):
        return pl.ds(block * ROWS + h * HALF, HALF)

    def part(block, h, p):
        return pl.ds(block * ROWS + h * HALF + p * PIECE, PIECE)

    def copy(*name):
        kind, tail = name[0], name[1:]
        if kind == "ix":
            src, dst, dev = X.at[rows(0, *tail)], X.at[rows(1, *tail)], xn
        elif kind == "iz":
            src, dst, dev = X.at[rows(0, *tail)], X.at[rows(2, *tail)], z2
        elif kind == "ixz":
            src, dst, dev = X.at[rows(2, *tail)], X.at[rows(3, *tail)], xn
        elif kind == "ty":
            src, dst, dev = Y.at[rows(0, *tail)], Y.at[rows(1, *tail)], yn
        elif kind == "tz":
            src, dst, dev = Y.at[rows(0, *tail)], Y.at[rows(2, *tail)], z1
        elif kind == "tyz":
            src, dst, dev = Y.at[rows(2, *tail)], Y.at[rows(3, *tail)], yn
        elif kind == "tc":
            src, dst, dev = Y.at[rows(*tail)], Y.at[rows(4 + tail[0], tail[1])], core
        elif kind == "ux":
            src, dst, dev = U.at[part(*tail)], RX.at[part(tail[0] // 2, *tail[1:])], xn
        elif kind == "uz":
            src, dst, dev = U.at[part(2, *tail)], RZ.at[part(0, *tail)], z2
        elif kind == "vc":
            src = V.at[pl.ds((4 + tail[0]) * ROWS, ROWS)]
            dst, dev = RC.at[pl.ds(tail[0] * ROWS, ROWS)], core
        elif kind == "vy":
            src, dst, dev = V.at[part(*tail)], RY.at[part(tail[0] // 2, *tail[1:])], yn
        elif kind == "vz":
            src, dst, dev = V.at[part(2, *tail)], RZ2.at[part(0, *tail)], z1
        else:
            src, dst, dev = ST.at[tail[0]], RS.at[tail[0]], peers[tail[0]]
        k = COPIES[name]
        return pltpu.make_async_remote_copy(src_ref=src, dst_ref=dst, send_sem=send.at[k], recv_sem=recv.at[k],
                                            device_id=(dev,), device_id_type=pl.DeviceIdType.MESH)

    start = lambda *name: copy(*name).start()
    arrived = lambda *name: copy(*name).wait_recv()

    for h in range(2):
        start("tc", 0, h)
    for h in range(2):
        start("ix", h)
        start("ty", h)
        start("iz", h)
        start("tz", h)

    def clear(k, carry):
        r = pl.ds(pl.multiple_of(k * 256, 256), 256)
        U[r, :] = jnp.zeros((256, WIDTH), jnp.float32)
        V[r, :] = jnp.zeros((256, WIDTH), jnp.float32)
        V[pl.ds(pl.multiple_of(4096 + k * 256, 256), 256), :] = jnp.zeros((256, WIDTH), jnp.float32)
        return carry

    lax.fori_loop(0, 16, clear, 0)
    sums[...] = jnp.zeros_like(sums)

    def spans(t):
        i, j = task_at(t)
        return pl.ds(pl.multiple_of(i * HALF, HALF), HALF), pl.ds(pl.multiple_of(j * ROWS, ROWS), ROWS)

    def logits(t):
        ri, rj = spans(t)
        return lax.dot_general(X[ri, :], Y[rj, :], NT_DIMS, preferred_element_type=jnp.float32)

    def weigh(diag_offset):
        s = S[...]
        m = s * ts2 + b2
        if diag_offset is not None:
            row = lax.broadcasted_iota(jnp.int32, s.shape, 0) + diag_offset
            on_diag = row == lax.broadcasted_iota(jnp.int32, s.shape, 1)
            m = jnp.where(on_diag, -m, m)
        e = jnp.exp2(-jnp.abs(m))
        q = 1.0 + e
        h = jnp.where(m >= 0, 1.0, e) * (1.0 / q)
        if diag_offset is not None:
            h = jnp.where(on_diag, -h, h)
        groups = lambda a: a.reshape(HALF // 8, 8, ROWS)
        sums[0] += jnp.sum(groups(h), axis=0)
        sums[1] += jnp.sum(groups(h * s), axis=0)
        sums[2] += jnp.sum(groups(jnp.maximum(m, 0.0)), axis=0)
        e3, q3 = groups(e), groups(q)
        p = e3[0]
        for k in range(1, HALF // 8):
            p = p * q3[k] + e3[k]
        sums[3] += jnp.log1p(p)
        return h.astype(jnp.bfloat16)

    def step(t, diag_offset=None):
        ri, rj = spans(t)
        hb = weigh(diag_offset)
        S[...] = logits(jnp.minimum(t + 1, len(TASKS) - 1))
        U[ri, :] += jnp.dot(hb, Y[rj, :], preferred_element_type=jnp.float32)
        V[rj, :] += lax.dot_general(hb, X[ri, :], TN_DIMS, preferred_element_type=jnp.float32)

    def add_into(dst, d0, src, s0, n):
        def body(k, carry):
            d = pl.ds(pl.multiple_of(d0 + k * 128, 128), 128)
            dst[d, :] += src[pl.ds(pl.multiple_of(s0 + k * 128, 128), 128), :]
            return carry
        lax.fori_loop(0, n // 128, body, 0)

    def at(block, h, p):
        return block * ROWS + h * HALF + p * PIECE

    first = {}
    for k, code in enumerate(TASKS):
        first.setdefault(("I", code // 8), k)
        first.setdefault(("T", code % 8), k)

    relays = {("ty", h): [("tc", 1, h)] for h in range(2)}
    relays.update({("tz", h): [("tyz", h), ("tc", 2, h)] for h in range(2)})
    relays.update({("tyz", h): [("tc", 3, h)] for h in range(2)})
    relays.update({("iz", h): [("ixz", h)] for h in range(2)})

    def perform(*name):
        kind, tail = name[0], name[1:]
        if name in relays:
            arrived(*name)
            for out in relays[name]:
                start(*out)
            return
        if kind == "uz":
            h, p = tail
            arrived("ux", 3, h, p)
            add_into(U, at(2, h, p), RX, at(1, h, p), PIECE)
        elif kind == "vy":
            q, h, p = tail
            if (h, p) == (0, 0):
                arrived("vc", q)
            add_into(V, at(q, h, p), RC, at(q, h, p), PIECE)
        elif kind == "vz":
            h, p = tail
            if (h, p) == (0, 0):
                arrived("vc", 2)
            arrived("vy", 3, h, p)
            add_into(V, at(2, h, p), RC, at(2, h, p), PIECE)
            add_into(V, at(2, h, p), RY, at(1, h, p), PIECE)
        start(*name)

    before = {}
    act = lambda k, fn: before.setdefault(k, []).append(fn)
    for k, *name in EVENTS:
        act(k, functools.partial(perform, *name))
    inputs = {("I", 2): [("ix", 0)], ("I", 3): [("ix", 1)], ("I", 6): [("ixz", 0)], ("I", 7): [("ixz", 1)]}
    inputs.update({("T", 4 + q): [("tc", q, 0), ("tc", q, 1)] for q in range(4)})
    for key, names in inputs.items():
        for name in names:
            act(max(first[key] - 1, 0), functools.partial(arrived, *name))

    def run_actions(k):
        for fn in before.get(k, []):
            fn()

    S[...] = logits(jnp.int32(0))

    def diag_body(t, carry):
        for k in (0, 1):
            if k in before:
                pl.when(t == k)(functools.partial(run_actions, k))
        step(t, t * HALF)
        return carry

    lax.fori_loop(0, 2, diag_body, 0)

    def body(t, carry):
        for k in sorted(before):
            if 2 <= k < 64:
                pl.when(t == k)(functools.partial(run_actions, k))
        step(t)
        return carry

    lax.fori_loop(2, 64, body, 0)
    run_actions(64)

    outs = []
    pieces = [(h, p) for h in range(2) for p in range(PARTS)]
    for h, p in pieces:
        arrived("ux", 1, h, p)
        add_into(U, at(0, h, p), RX, at(0, h, p), PIECE)
    arrived("vc", 0)
    for h, p in pieces:
        arrived("vy", 1, h, p)
        add_into(V, at(0, h, p), RC, at(0, h, p), PIECE)
        add_into(V, at(0, h, p), RY, at(0, h, p), PIECE)
    for h, p in pieces:
        for kind, dst, src, out in (("uz", U, RZ, u_out), ("vz", V, RZ2, v_out)):
            arrived(kind, h, p)
            add_into(dst, at(0, h, p), src, at(0, h, p), PIECE)
            r = part(0, h, p)
            outs.append(pltpu.make_async_copy(dst.at[r], out.at[r], local.at[2 + len(outs)]))
            outs[-1].start()

    kind_row = lax.broadcasted_iota(jnp.int32, (8, 128), 0)
    mine = jnp.zeros((8, 128), jnp.float32)
    for k in range(4):
        total = sums[k, :, 0:128]
        for c in range(128, ROWS, 128):
            total = total + sums[k, :, c:c + 128]
        mine = jnp.where(kind_row == k, jnp.sum(total, axis=0, keepdims=True), mine)
    for k in range(5):
        ST[k] = mine
        start("st", k)
        arrived("st", k)
        mine = mine + RS[k]
    st_out[...] = mine
    for out in outs:
        out.wait()
    for name in COPIES:
        copy(*name).wait_send()


def normalize_rows(emb):
    emb32 = emb.astype(jnp.float32)
    inv_norm = lax.rsqrt(jnp.sum(emb32 * emb32, axis=-1, keepdims=True))
    return emb32 * inv_norm, inv_norm


def project_back(unit_rows, inv_norm, grad_dir):
    radial = jnp.sum(unit_rows * grad_dir, axis=-1, keepdims=True)
    return (grad_dir - unit_rows * radial) * inv_norm


def solution(mesh):
    total_rows = ROWS * mesh.shape["dp"]
    f32 = lambda *shape: jax.ShapeDtypeStruct(shape, jnp.float32)
    acc = lambda n, dtype=jnp.float32: pltpu.VMEM((n, WIDTH), dtype)
    hbm = pl.BlockSpec(memory_space=pl.ANY)
    n_copies = len(COPIES)

    def local_fn(img_emb, txt_emb, log_temp, logit_bias):
        img_unit, img_inv = normalize_rows(img_emb)
        txt_unit, txt_inv = normalize_rows(txt_emb)
        temp_scale = jnp.exp(log_temp)
        scalars = jnp.stack([temp_scale * LOG2E, logit_bias * LOG2E])
        u_sum, v_sum, st = pl.pallas_call(
            pair_kernel,
            out_shape=[f32(ROWS, WIDTH), f32(ROWS, WIDTH), f32(8, 128)],
            in_specs=[pl.BlockSpec(memory_space=pltpu.SMEM), hbm, hbm],
            out_specs=[hbm, hbm, pl.BlockSpec(memory_space=pltpu.VMEM)],
            scratch_shapes=[
                acc(4096, jnp.bfloat16), acc(8192, jnp.bfloat16), acc(4096), acc(8192),
                acc(2048), acc(1024), acc(4096), acc(2048), acc(1024),
                pltpu.VMEM((HALF, ROWS), jnp.float32), pltpu.VMEM((4, 8, ROWS), jnp.float32),
                pltpu.VMEM((5, 8, 128), jnp.float32), pltpu.VMEM((5, 8, 128), jnp.float32),
                pltpu.SemaphoreType.DMA((n_copies,)), pltpu.SemaphoreType.DMA((n_copies,)),
                pltpu.SemaphoreType.DMA((2 + 4 * PARTS,)),
            ],
            compiler_params=pltpu.CompilerParams(collective_id=0, has_side_effects=True, vmem_limit_bytes=67043328),
        )(scalars, img_unit.astype(jnp.bfloat16), txt_unit.astype(jnp.bfloat16))
        sums = jnp.sum(st, axis=1) / total_rows
        loss = sums[3] + LN2 * sums[2]
        grad_img = project_back(img_unit, img_inv, temp_scale * u_sum)
        grad_txt = project_back(txt_unit, txt_inv, temp_scale * v_sum)
        return loss, grad_img, grad_txt, temp_scale * sums[1], sums[0]

    return jax.shard_map(
        local_fn,
        mesh=mesh,
        in_specs=(P("dp", None), P("dp", None), P(), P()),
        out_specs=(P(), P("dp", None), P("dp", None), P(), P()),
        check_vma=False,
    )
```

time: 1480 us -> 298 us (0.20)
  waiting for transfers between devices: 900 us -> 0 us
  matrix products: 418 us -> 0 us
  Pallas kernels: 0 us -> 275 us
  other arithmetic: 75.6 us -> 14.5 us
  blocking collectives: 48.3 us -> 0 us
  local copies, waits for them, and re-layouts: 31.5 us -> 1.51 us
    ppermute x63 -> x0, waiting for transfers between devices: 900 us -> none  [the longest x31 550 us: visit_step(): txt_blk = lax.ppermute(txt_blk, 'dp', shift_pairs)]
    dot_general x96 -> x0, matrix products: 418 us -> none  [the longest x32 199 us: pair_terms(): jnp.einsum('id,jd->ij', img_b, txt_blk, preferred_element_type=jnp.float32)]
    pallas_call x0 -> x1, Pallas kernels: none -> 275 us  [local_fn(): pl.pallas_call(pair_kernel, out_shape=[f32(ROWS, WIDTH), f32(ROWS, WIDTH)...]
    add x31 -> x0, other arithmetic: 60.4 us -> none  [visit_step(): stat_sums + new_sums]
    psum x1 -> x0, blocking collectives: 48.3 us -> none  [local_fn(): stat_sums = lax.psum(loop_state[3], 'dp') / total_rows]
    while x155 -> x0, local copies, waits for them, and re-layouts: 30.8 us -> none
  transfers between devices with their start and end apart: 63 -> 0, of which waited for: 62 -> 0; matrix products, arithmetic and copies ran while one was open for 24% -> 0% of each run, Pallas kernels for 0% -> 0%
where the time goes in v1:
time: 298 us
  Pallas kernels  275 us (92%)
  other arithmetic  14.5 us (5%)
  between operations  6.41 us (2%)
    pallas_call x1, Pallas kernels, local_fn(): pl.pallas_call(pair_kernel, out_shape=[f32(ROWS, WIDTH), f32(ROWS, WIDTH)...  275 us

profile of v1, /device:TPU:0, one launch (start us, length us, event | category | flops | bytes accessed | tf_op | source)
XLA Modules:
  0.0 297.6 jit_solution(12940875323649649378)
XLA Ops:
  0.6 0.0 copy-start
  2.1 0.6 pad_maximum_fusion.sc_ref
  2.6 0.0 copy-start.2
  2.7 1.6 fusion.9
  4.3 0.0 copy-start.6
  4.3 1.5 fusion.13
  5.8 0.0 copy-done
  5.8 0.0 copy-start.8
  5.8 1.3 fusion.2.yin
  7.1 0.0 copy-done.6
  7.1 0.0 copy-done.8
  7.1 0.0 copy-done.2
  7.1 1.3 fusion.5.xin
  8.3 275.1 %shard_map.83 = (f32[1024,512]{1,0:T(8,128)}, f32[1024,512]{1,0:T(8,128)}, f32[8,128]{1,0:T(8,128)}) custom-call(f32[2]{0:T(128)} %pad_maximum_fusion.sc_ref, bf16[1024,512]{1,0:T(8,128)(2,1)} %fusion.5.xin, bf16[1024,512]{1,0:T(8,128)(2,1)} %fusion.2.yin), custom_call_target="tpu_custom_call" | custom-call | tf_op jit(solution)/shard_map/pallas_call | solution.py:356
  283.4 0.8 reduce_sum.47
  284.2 0.6 fusion.14
  286.8 0.0 copy-start.1
  286.8 0.0 copy-start.5
  286.8 0.0 copy-start.9
  286.8 4.0 %fusion.6 = (f32[1024]{0:T(1024)S(1)}, f32[1024]{0:T(1024)S(1)}) fusion(bf16[1024,512]{1,0:T(8,128)(2,1)} %param.4, f32[1024,512]{1,0:T(8,128)} %get-tuple-element.9, f32[]{:T(128)S(6)} %exp.3, f32[1024]{0:T(1024)} %copy-done.6, f32[1024,512]{1,0:T(8,128)} %get-tuple-element.10, f32[1024]{0:T(1024)} %copy-done.8, bf16[1024,512]{1,0:T(8,128)(2,1)} %param.5), kind=kLoop, calls=%fused_computation.10 | loop fusion | flops 5240832 | bytes 6307844 | tf_op jit(solution)/shard_map/reduce_sum | solution.py:340
  290.8 0.0 copy-done.1
  290.8 0.0 copy-done.5
  290.8 0.0 copy-done.9
  290.8 0.0 copy-start.3
  290.9 0.0 copy-start.4
  290.9 0.0 copy-start.7
  290.9 1.8 fusion.12
  292.7 0.0 copy-done.3
  292.7 0.9 copy-done.4
  293.5 0.0 copy-done.7
  293.5 1.8 fusion.8
  (3 shorter events, 0.0 us)
Async XLA Ops:
  0.6 5.1 %copy-start = (bf16[1024,512]{1,0:T(8,128)(2,1)S(1)}, bf16[1024,512]{1,0:T(8,128)(2,1)}, u32[]{:S(2)}) copy-start(bf16[1024,512]{1,0:T(8,128)(2,1)} %param.5) | copy-start | bytes 3145732
  2.6 4.4 %copy-start.2 = (bf16[1024,512]{1,0:T(8,128)(2,1)S(1)}, bf16[1024,512]{1,0:T(8,128)(2,1)}, u32[]{:S(2)}) copy-start(bf16[1024,512]{1,0:T(8,128)(2,1)} %param.4) | copy-start | bytes 3145732
  4.3 2.8 copy-start.6
  5.8 1.3 copy-start.8
  286.8 4.0 %copy-start.1 = (bf16[1024,512]{1,0:T(8,128)(2,1)S(1)}, bf16[1024,512]{1,0:T(8,128)(2,1)}, u32[]{:S(2)}) copy-start(bf16[1024,512]{1,0:T(8,128)(2,1)} %param.5) | copy-start | bytes 3145732
  286.8 4.0 %copy-start.5 = (f32[1024,512]{1,0:T(8,128)S(1)}, f32[1024,512]{1,0:T(8,128)}, u32[]{:S(2)}) copy-start(f32[1024,512]{1,0:T(8,128)} %get-tuple-element.10) | copy-start | bytes 6291460
  286.8 4.0 %copy-start.9 = (f32[1024]{0:T(1024)S(1)}, f32[1024]{0:T(1024)}, u32[]{:S(2)}) copy-start(f32[1024]{0:T(1024)} %copy-done.8) | copy-start | bytes 12292
  290.8 1.8 copy-start.3
  290.9 2.7 copy-start.4
  290.9 2.7 copy-start.7
